TPU v7x, 32 devices: a whole 2x2x4 slice. The times are simulated.
32 devices in a mesh: ens: 2 (over y), box: 4 (over z), slab: 4 (over x, core).
Axes of the slice: x: 2, y: 2, z: 4, core: 2. Of those that a mesh axis runs over, the one named last changes fastest.
Arguments:
- pressure_now: float32 [4, 64, 64, 256], P('ens', 'box', 'slab'), parts along dimension 0, may hold values from -6 to 6
- pressure_prev: float32 [4, 64, 64, 256], P('ens', 'box', 'slab'), parts along dimension 0, may hold values from -6 to 6
- courant_sq: float32 [64, 64, 256], P('box', 'slab'), may hold values from 0.04 to 0.28
- member_profiles: float32 [8, 64], replicated, may hold values from -0.15 to 0.15
- member_ids: int32 [4], P('ens'), parts along dimension 0, may hold values from 0 to 7, as said below
- stored_slabs: float32 [8, 16, 6144], P('slab'), may hold values from -6 to 6
- slab_home: int32 [2], P('ens'), parts along dimension 0, may hold values from 0 to 7
- interp_weights: float32 [2, 16], replicated, may hold values from -1.5 to 1.5
- surface_cells: int32 [6, 1024], replicated, may hold values from 0 to 1048575, as said below
Outputs:
- pressure_next: float32 [4, 64, 64, 256], P('ens', 'box', 'slab'), parts along dimension 0
- pressure_last: float32 [4, 64, 64, 256], P('ens', 'box', 'slab'), parts along dimension 0
There are 2 independent parts, one for each index of `ens`. A program takes and returns all parts, laid end to end along the dimension named above; an argument that names none is the same for every part. Nothing has to cross between parts.
Inputs may be any that keep to these rules, and one draw needn't show every extreme that they name: `surface_cells`: row f lists 1024 cells, flat index (x 64 + z) * 256 + y, on one face of the box surface 0 cells inside the grid: x low, x high, z low, z high, y low, y high in this order; the other two coordinates lie on the surface; on every face other than the two depth faces, every depth of the surface occurs; cells may repeat. `slab_home`: block k is stored on the slab device k // 2, in its slot k % 2. `member_ids`: the members' profiles are all different.
All inputs are finite; a program needn't handle non-finite values.
Results may differ from a plain program's by a relative error of at most 0.000098.
Values sent between devices are 32-bit elements; how exact they have to be, the bound alone decides.
A program may use at most 64 MiB of HBM per device.

v0:
```python
import jax
import jax.numpy as jnp
from jax import lax
from jax.sharding import PartitionSpec as P


def extended(array, sides, width):
    for axis, dim in sides:
        peers, length = (lax.axis_size(axis), array.shape[dim])
        up = [(i, (i + 1) % peers) for i in range(peers - 1)]
        down = [(j, i) for i, j in up]
        last = lax.slice_in_dim(array, length - width, length, axis=dim)
        leading = lax.slice_in_dim(array, 0, width, axis=dim)
        before = lax.ppermute(last, axis, up)
        after = lax.ppermute(leading, axis, down)
        array = jnp.concatenate([before, array, after], axis=dim)
    return array


def laplace(ext):
    inner = ext[:, 1:-1, 1:-1, :]
    beside = ext[:, 2:, 1:-1, :] + ext[:, :-2, 1:-1, :]
    beside = beside + ext[:, 1:-1, 2:, :] + ext[:, 1:-1, :-2, :]
    padded = jnp.pad(inner, ((0, 0), (0, 0), (0, 0), (1, 1)))
    beside = beside + padded[:, :, :, 2:] + padded[:, :, :, :-2]
    return beside - 6.0 * inner


def inject(field, cells, point_values, anchor_x, anchor_z, total_z):
    extent_x, extent_z, depth_y = (field.shape[1], field.shape[2], field.shape[3])
    plane = total_z * depth_y
    cell_x = cells // plane
    remain = cells % plane
    cell_z = remain // depth_y
    cell_y = remain % depth_y
    local_x = cell_x - anchor_x
    local_z = cell_z - anchor_z
    inside = (local_x >= 0) & (local_x < extent_x) & (local_z >= 0) & (local_z < extent_z)
    volume = extent_x * extent_z * depth_y
    target = jnp.where(inside, (local_x * extent_z + local_z) * depth_y + cell_y, volume)
    source = jnp.zeros((volume,), jnp.float32).at[target].add(point_values, mode="drop")
    return field + source.reshape(extent_x, extent_z, depth_y)[None]


def on_device(
    pressure_now,
    pressure_prev,
    courant_sq,
    member_profiles,
    member_ids,
    stored_slabs,
    slab_home,
    interp_weights,
    surface_cells,
):
    members, width_x, width_z, depth_y = pressure_now.shape
    total_z = width_z * lax.axis_size("slab")
    start_x = lax.axis_index("box") * width_x
    start_z = lax.axis_index("slab") * width_z
    profiles = member_profiles.shape[0]
    choose = (member_ids[:, None] == jnp.arange(profiles, dtype=jnp.int32)[None, :]).astype(
        jnp.float32
    )
    profile_all = jnp.dot(choose, member_profiles, precision=lax.Precision.HIGHEST)
    profile_here = lax.dynamic_slice_in_dim(profile_all, start_z, width_z, 1)
    coef = courant_sq[None] * (1.0 + profile_here[:, None, :, None])
    slots = stored_slabs.shape[0]
    home = slab_home[0]
    is_owner = lax.axis_index("slab") == home // slots
    mine = lax.dynamic_index_in_dim(stored_slabs, home % slots, 0, keepdims=False)
    partial_values = jnp.dot(interp_weights, mine, precision=lax.Precision.HIGHEST)
    offered = jnp.where(is_owner, partial_values, jnp.zeros_like(partial_values))
    values = lax.psum(offered, "slab")
    cells = surface_cells.reshape(-1)
    count = interp_weights.shape[0]
    prev, now = (pressure_prev, pressure_now)
    for step in range(count):
        ext = extended(now, (("box", 1), ("slab", 2)), 1)
        nxt = 2.0 * now - prev + coef * laplace(ext)
        nxt = inject(nxt, cells, values[step], start_x, start_z, total_z)
        prev, now = (now, nxt)
    return (now, prev)


def solution(mesh):
    in_specs = (
        P("ens", "box", "slab", None),
        P("ens", "box", "slab", None),
        P("box", "slab", None),
        P(),
        P("ens"),
        P("slab", None, None),
        P("ens"),
        P(),
        P(),
    )
    out_specs = (P("ens", "box", "slab", None), P("ens", "box", "slab", None))
    return jax.shard_map(
        on_device, mesh=mesh, in_specs=in_specs, out_specs=out_specs, check_vma=False
    )
```

profile of v0, /device:TPU:0, one launch (start us, length us, event | category | flops | bytes accessed | tf_op | source)
XLA Modules:
  0.0 108.8 jit_solution(6065750017297019400)
XLA Ops:
  0.7 0.9 fusion.31
  1.5 4.9 %collective-permute-start.1 = (f32[2,1,16,256]{3,2,1,0:T(8,128)S(1)}, f32[2,1,16,256]{3,2,1,0:T(8,128)S(1)}, u32[]{:S(2)}, u32[]{:S(2)}) collective-permute-start(f32[2,1,16,256]{3,2,1,0:T(8,128)S(1)} %get-tuple-element.9), channel_id=1, source_target_pairs={{0,4},{4,8},{8,12},{1,5},{5,9},{9,13},{2,6},{6,10},{10,14},{3,7},{... | collective-permute-start | bytes 98312 | tf_op jit(solution)/shard_map/ppermute | solution.py:14
  6.5 1.3 %collective-permute-start = (f32[2,1,16,256]{3,2,1,0:T(8,128)S(1)}, f32[2,1,16,256]{3,2,1,0:T(8,128)S(1)}, u32[]{:S(2)}, u32[]{:S(2)}) collective-permute-start(f32[2,1,16,256]{3,2,1,0:T(8,128)S(1)} %get-tuple-element.8), channel_id=1, source_target_pairs={{4,0},{8,4},{12,8},{5,1},{9,5},{13,9},{6,2},{10,6},{14,10},{7,3},{... | collective-permute-start | bytes 98312 | tf_op jit(solution)/shard_map/ppermute | solution.py:15
  8.5 1.0 fusion
  9.5 11.1 %psum.7 = f32[2,6144]{1,0:T(2,128)S(1)} all-reduce(f32[2,6144]{1,0:T(2,128)S(1)} %fusion), channel_id=1, replica_groups=mesh['ens'=2,'box'=4,'slab'=4] {'slab'}, use_global_device_ids=true, to_apply=%region_0.1 | all-reduce | flops 12288 | bytes 98304 | tf_op jit(solution)/shard_map/psum | solution.py:73
  20.6 0.6 fusion.32
  21.3 0.1 copy-done.6
  21.4 0.4 compare_select_fusion
  21.9 0.2 copy-done.8
  22.1 0.2 fusion.24
  22.5 1.4 %collective-permute-start.2 = (f32[2,18,1,256]{3,2,1,0:T(1,128)S(1)}, f32[2,18,1,256]{3,2,1,0:T(1,128)S(1)}, u32[]{:S(2)}, u32[]{:S(2)}) collective-permute-start(f32[2,18,1,256]{3,2,1,0:T(1,128)S(1)} %get-tuple-element.4), channel_id=1, source_target_pairs={{1,0},{2,1},{3,2},{5,4},{6,5},{7,6},{9,8},{10,9},{11,10},{13,12},{... | collective-permute-start | bytes 110600 | tf_op jit(solution)/shard_map/ppermute | solution.py:15
  23.9 3.6 %collective-permute-start.3 = (f32[2,18,1,256]{3,2,1,0:T(1,128)S(1)}, f32[2,18,1,256]{3,2,1,0:T(1,128)}, u32[]{:S(2)}, u32[]{:S(2)}) collective-permute-start(f32[2,18,1,256]{3,2,1,0:T(1,128)S(1)} %get-tuple-element.5), channel_id=1, source_target_pairs={{0,1},{1,2},{2,3},{4,5},{5,6},{6,7},{8,9},{9,10},{10,11},{12,13},{... | collective-permute-start | bytes 110600 | tf_op jit(solution)/shard_map/ppermute | solution.py:14
  27.6 32.6 %scatter_custom_fusion = f32[65536]{0:T(1024)S(1)} fusion(s32[6144]{0:T(1024)S(1)} %bitcast.21, f32[6144]{0:T(1024)S(1)} %bitcast.24, f32[]{:T(128)} %constant.98.clone.1), kind=kCustom, calls=%fused_computation.43 | custom fusion | flops 6144 | bytes 262148 | tf_op jit(solution)/shard_map/scatter-add | solution.py:41
  60.3 0.6 copy-done.5
  61.0 0.2 copy-done.3
  61.2 1.2 %fusion.2 = f32[2,16,16,256]{3,2,1,0:T(8,128)S(1)} fusion(f32[2,16,16,256]{3,2,1,0:T(8,128)S(1)} %copy-done.1, f32[2,18,16,256]{3,2,1,0:T(8,128)S(1)} %constant_dynamic-update-slice_fusion, f32[2,18,1,256]{3,2,1,0:T(1,128)} %collective-permute-done.3, f32[2,18,1,256]{3,2,1,0:T(1,128)} %copy-done.5, f32[2,1,16,256]{3,2,1,0:T(8,128)S(1)} %collective-permute-done.1, ...), kind=kLoop, calls=%fused_computation.11 | loop fusion | flops 2228224 | bytes 2826368 | tf_op jit(solution)/shard_map/add | solution.py:42
  62.4 1.3 %collective-permute-start.4 = (f32[2,1,16,256]{3,2,1,0:T(8,128)S(1)}, f32[2,1,16,256]{3,2,1,0:T(8,128)S(1)}, u32[]{:S(2)}, u32[]{:S(2)}) collective-permute-start(f32[2,1,16,256]{3,2,1,0:T(8,128)S(1)} %get-tuple-element.7), channel_id=1, source_target_pairs={{4,0},{8,4},{12,8},{5,1},{9,5},{13,9},{6,2},{10,6},{14,10},{7,3},{... | collective-permute-start | bytes 98312 | tf_op jit(solution)/shard_map/ppermute | solution.py:15
  63.7 4.9 %collective-permute-start.5 = (f32[2,1,16,256]{3,2,1,0:T(8,128)S(1)}, f32[2,1,16,256]{3,2,1,0:T(8,128)S(1)}, u32[]{:S(2)}, u32[]{:S(2)}) collective-permute-start(f32[2,1,16,256]{3,2,1,0:T(8,128)S(1)} %get-tuple-element.6), channel_id=1, source_target_pairs={{0,4},{4,8},{8,12},{1,5},{5,9},{9,13},{2,6},{6,10},{10,14},{3,7},{... | collective-permute-start | bytes 98312 | tf_op jit(solution)/shard_map/ppermute | solution.py:14
  68.7 0.3 collective-permute-done.4
  68.9 1.3 %collective-permute-done.5 = f32[2,1,16,256]{3,2,1,0:T(8,128)S(1)} collective-permute-done((f32[2,1,16,256]{3,2,1,0:T(8,128)S(1)}, f32[2,1,16,256]{3,2,1,0:T(8,128)S(1)}, u32[]{:S(2)}, u32[]{:S(2)}) %collective-permute-start.5) | collective-permute-done | bytes 32800 | tf_op jit(solution)/shard_map/ppermute | solution.py:14
  70.3 1.3 %collective-permute-start.6 = (f32[2,18,1,256]{3,2,1,0:T(1,128)S(1)}, f32[2,18,1,256]{3,2,1,0:T(1,128)S(1)}, u32[]{:S(2)}, u32[]{:S(2)}) collective-permute-start(f32[2,18,1,256]{3,2,1,0:T(1,128)S(1)} %get-tuple-element.2), channel_id=1, source_target_pairs={{1,0},{2,1},{3,2},{5,4},{6,5},{7,6},{9,8},{10,9},{11,10},{13,12},{... | collective-permute-start | bytes 110600 | tf_op jit(solution)/shard_map/ppermute | solution.py:15
  71.6 3.0 %collective-permute-start.7 = (f32[2,18,1,256]{3,2,1,0:T(1,128)S(1)}, f32[2,18,1,256]{3,2,1,0:T(1,128)S(1)}, u32[]{:S(2)}, u32[]{:S(2)}) collective-permute-start(f32[2,18,1,256]{3,2,1,0:T(1,128)S(1)} %get-tuple-element.3), channel_id=1, source_target_pairs={{0,1},{1,2},{2,3},{4,5},{5,6},{6,7},{8,9},{9,10},{10,11},{12,13},{... | collective-permute-start | bytes 110600 | tf_op jit(solution)/shard_map/ppermute | solution.py:14
  74.6 32.8 %scatter_custom_fusion.1 = f32[65536]{0:T(1024)S(1)} fusion(s32[6144]{0:T(1024)} %bitcast.22, f32[6144]{0:T(1024)} %bitcast.23, f32[]{:T(128)} %constant.98.clone.1), kind=kCustom, calls=%fused_computation.41 | custom fusion | flops 6144 | bytes 262656 | tf_op jit(solution)/shard_map/scatter-add | solution.py:41
  107.5 1.3 %fusion.4 = f32[2,16,16,256]{3,2,1,0:T(8,128)} fusion(f32[2,16,16,256]{3,2,1,0:T(8,128)S(1)} %fusion.2, f32[2,18,1,256]{3,2,1,0:T(1,128)S(1)} %collective-permute-done.7, f32[2,1,16,256]{3,2,1,0:T(8,128)S(1)} %collective-permute-done.4, f32[2,1,16,256]{3,2,1,0:T(8,128)S(1)} %collective-permute-done.5, f32[2,18,1,256]{3,2,1,0:T(1,128)S(1)} %collective-permute-done.6, ...), kind=kLoop, calls=%fused_computation.13 | loop fusion | flops 2752512 | bytes 2236544 | tf_op jit(solution)/shard_map/add | solution.py:42
  (32 shorter events, 0.5 us)
Async XLA Ops:
  0.6 7.9 %copy-start = (f32[2,16,6144]{2,1,0:T(8,128)S(1)}, f32[2,16,6144]{2,1,0:T(8,128)}, u32[]{:S(2)}) copy-start(f32[2,16,6144]{2,1,0:T(8,128)} %param.14) | copy-start | bytes 2359300
  0.6 21.7 %copy-start.1 = (f32[2,16,16,256]{3,2,1,0:T(8,128)S(1)}, f32[2,16,16,256]{3,2,1,0:T(8,128)}, u32[]{:S(2)}) copy-start(f32[2,16,16,256]{3,2,1,0:T(8,128)} %param.9) | copy-start | bytes 1572868
  1.5 20.7 %collective-permute-start.1 = (f32[2,1,16,256]{3,2,1,0:T(8,128)S(1)}, f32[2,1,16,256]{3,2,1,0:T(8,128)S(1)}, u32[]{:S(2)}, u32[]{:S(2)}) collective-permute-start(f32[2,1,16,256]{3,2,1,0:T(8,128)S(1)} %get-tuple-element.9), channel_id=1, source_target_pairs={{0,4},{4,8},{8,12},{1,5},{5,9},{9,13},{2,6},{6,10},{10,14},{3,7},{... | collective-permute-start | bytes 98312 | tf_op jit(solution)/shard_map/ppermute | solution.py:14
  6.5 15.9 %collective-permute-start = (f32[2,1,16,256]{3,2,1,0:T(8,128)S(1)}, f32[2,1,16,256]{3,2,1,0:T(8,128)S(1)}, u32[]{:S(2)}, u32[]{:S(2)}) collective-permute-start(f32[2,1,16,256]{3,2,1,0:T(8,128)S(1)} %get-tuple-element.8), channel_id=1, source_target_pairs={{4,0},{8,4},{12,8},{5,1},{9,5},{13,9},{6,2},{10,6},{14,10},{7,3},{... | collective-permute-start | bytes 98312 | tf_op jit(solution)/shard_map/ppermute | solution.py:15
  20.6 0.8 copy-start.6
  21.4 0.7 copy-start.8
  21.4 0.7 copy-start.9
  22.1 5.5 %copy-start.7 = (s32[6144,1]{0,1:T(1,128)}, s32[6144,1]{0,1:T(1,128)S(1)}, u32[]{:S(2)}) copy-start(s32[6144,1]{0,1:T(1,128)S(1)} %compare_select_fusion) | copy-start | bytes 73732
  22.4 38.6 %copy-start.4 = (f32[2,16,16,256]{3,2,1,0:T(8,128)S(1)}, f32[2,16,16,256]{3,2,1,0:T(8,128)}, u32[]{:S(2)}) copy-start(f32[2,16,16,256]{3,2,1,0:T(8,128)} %param.10) | copy-start | bytes 1572868
  22.5 37.9 %collective-permute-start.2 = (f32[2,18,1,256]{3,2,1,0:T(1,128)S(1)}, f32[2,18,1,256]{3,2,1,0:T(1,128)S(1)}, u32[]{:S(2)}, u32[]{:S(2)}) collective-permute-start(f32[2,18,1,256]{3,2,1,0:T(1,128)S(1)} %get-tuple-element.4), channel_id=1, source_target_pairs={{1,0},{2,1},{3,2},{5,4},{6,5},{7,6},{9,8},{10,9},{11,10},{13,12},{... | collective-permute-start | bytes 110600 | tf_op jit(solution)/shard_map/ppermute | solution.py:15
  23.9 37.1 %collective-permute-start.3 = (f32[2,18,1,256]{3,2,1,0:T(1,128)S(1)}, f32[2,18,1,256]{3,2,1,0:T(1,128)}, u32[]{:S(2)}, u32[]{:S(2)}) collective-permute-start(f32[2,18,1,256]{3,2,1,0:T(1,128)S(1)} %get-tuple-element.5), channel_id=1, source_target_pairs={{0,1},{1,2},{2,3},{4,5},{5,6},{6,7},{8,9},{9,10},{10,11},{12,13},{... | collective-permute-start | bytes 110600 | tf_op jit(solution)/shard_map/ppermute | solution.py:14
  60.2 1.0 copy-start.3
  60.3 0.6 copy-start.5
  62.4 45.1 %copy-start.2 = (f32[2,16,16,256]{3,2,1,0:T(8,128)}, f32[2,16,16,256]{3,2,1,0:T(8,128)S(1)}, u32[]{:S(2)}) copy-start(f32[2,16,16,256]{3,2,1,0:T(8,128)S(1)} %fusion.2) | copy-start | bytes 1572868
  62.4 6.5 %collective-permute-start.4 = (f32[2,1,16,256]{3,2,1,0:T(8,128)S(1)}, f32[2,1,16,256]{3,2,1,0:T(8,128)S(1)}, u32[]{:S(2)}, u32[]{:S(2)}) collective-permute-start(f32[2,1,16,256]{3,2,1,0:T(8,128)S(1)} %get-tuple-element.7), channel_id=1, source_target_pairs={{4,0},{8,4},{12,8},{5,1},{9,5},{13,9},{6,2},{10,6},{14,10},{7,3},{... | collective-permute-start | bytes 98312 | tf_op jit(solution)/shard_map/ppermute | solution.py:15
  63.7 6.5 %collective-permute-start.5 = (f32[2,1,16,256]{3,2,1,0:T(8,128)S(1)}, f32[2,1,16,256]{3,2,1,0:T(8,128)S(1)}, u32[]{:S(2)}, u32[]{:S(2)}) collective-permute-start(f32[2,1,16,256]{3,2,1,0:T(8,128)S(1)} %get-tuple-element.6), channel_id=1, source_target_pairs={{0,4},{4,8},{8,12},{1,5},{5,9},{9,13},{2,6},{6,10},{10,14},{3,7},{... | collective-permute-start | bytes 98312 | tf_op jit(solution)/shard_map/ppermute | solution.py:14
  70.3 37.2 %collective-permute-start.6 = (f32[2,18,1,256]{3,2,1,0:T(1,128)S(1)}, f32[2,18,1,256]{3,2,1,0:T(1,128)S(1)}, u32[]{:S(2)}, u32[]{:S(2)}) collective-permute-start(f32[2,18,1,256]{3,2,1,0:T(1,128)S(1)} %get-tuple-element.2), channel_id=1, source_target_pairs={{1,0},{2,1},{3,2},{5,4},{6,5},{7,6},{9,8},{10,9},{11,10},{13,12},{... | collective-permute-start | bytes 110600 | tf_op jit(solution)/shard_map/ppermute | solution.py:15
  71.6 35.9 %collective-permute-start.7 = (f32[2,18,1,256]{3,2,1,0:T(1,128)S(1)}, f32[2,18,1,256]{3,2,1,0:T(1,128)S(1)}, u32[]{:S(2)}, u32[]{:S(2)}) collective-permute-start(f32[2,18,1,256]{3,2,1,0:T(1,128)S(1)} %get-tuple-element.3), channel_id=1, source_target_pairs={{0,1},{1,2},{2,3},{4,5},{5,6},{6,7},{8,9},{9,10},{10,11},{12,13},{... | collective-permute-start | bytes 110600 | tf_op jit(solution)/shard_map/ppermute | solution.py:14
where the time goes:
time: 110 us; the launch traced here: 109 us
  other arithmetic  68.5 us (62%)
  starting transfers between devices  21.8 us (20%)
  blocking collectives  11.1 us (10%)
  local copies, waits for them, and re-layouts  3.01 us (3%)
  between operations  1.6 us (1%)
  waiting for transfers between devices  1.59 us (1%)
  matrix products  1.2 us (1%)
    scatter-add x2, other arithmetic, inject(): jnp.zeros((volume,), jnp.float32).at[target].add(point_values, mode='drop')  65.4 us
    ppermute x4, starting transfers between devices, extended(): before = lax.ppermute(last, axis, up)  16.5 us
    psum x1, blocking collectives, on_device(): values = lax.psum(offered, 'slab')  11.1 us
    ppermute x4, starting transfers between devices, extended(): after = lax.ppermute(leading, axis, down)  5.3 us
    add x2, other arithmetic, inject(): return field + source.reshape(extent_x, extent_z, depth_y)[None]  2.5 us
  transfers between devices with their start and end apart: 8, of which 2 were waited for; matrix products, arithmetic and copies ran while one was open for 62% of the time, Pallas kernels for 0%

commit v1 on v0

v1 whole, which is shorter than its diff:
```python
import functools

import jax
import jax.numpy as jnp
from jax import lax
from jax.experimental import pallas as pl
from jax.experimental.pallas import tpu as pltpu
from jax.sharding import PartitionSpec as P

F32, BF16, I32 = jnp.float32, jnp.bfloat16, jnp.int32
MESH = pl.DeviceIdType.MESH


def iota(shape, dim):
    return lax.broadcasted_iota(I32, shape, dim)


def quotient(values, divisor):
    if divisor & (divisor - 1) == 0:
        return lax.shift_right_logical(values, divisor.bit_length() - 1)
    return lax.div(values, jnp.full_like(values, divisor))


def split3(v):
    high = v.astype(BF16).astype(F32)
    rest = v - high
    mid = rest.astype(BF16).astype(F32)
    return high, mid, rest - mid


def place(rows, row_of, valid, per_step, cols, col_of):
    hit = (iota((rows, row_of.shape[1]), 0) == row_of) & valid
    parts = []
    for v in per_step:
        for term in split3(v):
            parts.append(jnp.where(hit, term, 0.0).astype(BF16))
    left = jnp.concatenate(parts, axis=0)
    right = jnp.where(iota((cols, col_of.shape[1]), 0) == col_of, 1.0, 0.0).astype(BF16)
    sums = lax.dot_general(left, right, (((1,), (1,)), ((), ())), preferred_element_type=F32)
    out = []
    for t in range(len(per_step)):
        a = sums[3 * t * rows : (3 * t + 1) * rows]
        b = sums[(3 * t + 1) * rows : (3 * t + 2) * rows]
        c = sums[(3 * t + 2) * rows : (3 * t + 3) * rows]
        out.append(a + (b + c))
    return out


def kernel(dims, ids, home, prof, weights, cells, now_h, prev_h, cour_h, slabs_h, two, one,
           now, prev, coef, slabs, zsend, xghost, zghost, vsend, vrecv,
           load_sem, hs_sem, hr_sem, vs_sem, vr_sem):
    members, wx, wz, ny, slots, length, pts, n_box, n_slab = dims
    steps = 2
    block = wx * wz
    box, slab = lax.axis_index("box"), lax.axis_index("slab")
    loads = [
        pltpu.make_async_copy(src, dst, load_sem.at[i])
        for i, (src, dst) in enumerate(((now_h, now), (slabs_h, slabs), (prev_h, prev), (cour_h, coef.at[pl.ds(0, block)])))
    ]
    for c in loads:
        c.start()

    barrier = pltpu.get_barrier_semaphore()

    def greet(target):
        pl.semaphore_signal(barrier, inc=1, device_id=target, device_id_type=MESH)

    @pl.when(box > 0)
    def _():
        greet({"box": box - 1})

    @pl.when(box < n_box - 1)
    def _():
        greet({"box": box + 1})

    for d in range(1, n_slab):
        greet({"slab": lax.rem(slab + d, n_slab)})
    box_peers = jnp.where(box > 0, 1, 0) + jnp.where(box < n_box - 1, 1, 0)
    pl.semaphore_wait(barrier, n_slab - 1 + box_peers)

    def halo(field, r, way):
        if way < 2:
            plane = wx - 1 if way == 0 else 0
            peer = {"box": box + 1 if way == 0 else box - 1}
            return [
                pltpu.make_async_remote_copy(
                    field.at[pl.ds((m * wx + plane) * wz, wz)], xghost.at[r, way, m],
                    hs_sem.at[r, way, m], hr_sem.at[r, way, m], device_id=peer, device_id_type=MESH)
                for m in range(members)
            ]
        peer = {"slab": slab + 1 if way == 2 else slab - 1}
        return [
            pltpu.make_async_remote_copy(
                zsend.at[r, way - 2], zghost.at[r, way - 2], hs_sem.at[r, way, 0], hr_sem.at[r, way, 0],
                device_id=peer, device_id_type=MESH)
        ]

    sends_to = (box < n_box - 1, box > 0, slab < n_slab - 1, slab > 0)
    hears_from = (box > 0, box < n_box - 1, slab > 0, slab < n_slab - 1)

    def send_halos(field, r):
        for way in (0, 1):
            @pl.when(sends_to[way])
            def _(way=way):
                for c in halo(field, r, way):
                    c.start()
        for way in (2, 3):
            row = wz - 1 if way == 2 else 0
            for m in range(members):
                for x in range(wx):
                    zsend[r, way - 2, m, x : x + 1, :] = field[pl.ds((m * wx + x) * wz + row, 1), :]

            @pl.when(sends_to[way])
            def _(way=way):
                for c in halo(field, r, way):
                    c.start()

    def add_halos(field, r, out):
        for way in (0, 1):
            plane = 0 if way == 0 else wx - 1

            @pl.when(hears_from[way])
            def _(way=way, plane=plane):
                for m, c in enumerate(halo(field, r, way)):
                    c.wait_recv()
                for m in range(members):
                    rows = pl.ds((m * wx + plane) * wz, wz)
                    out[rows, :] += coef[rows, :] * xghost[r, way, m]
        for way in (2, 3):
            row = 0 if way == 2 else wz - 1

            @pl.when(hears_from[way])
            def _(way=way, row=row):
                for c in halo(field, r, way):
                    c.wait_recv()
                for m in range(members):
                    for x in range(wx):
                        at = pl.ds((m * wx + x) * wz + row, 1)
                        out[at, :] += coef[at, :] * zghost[r, way - 2, m, x : x + 1, :]

    def end_sends(field, r):
        for way in range(4):
            @pl.when(sends_to[way])
            def _(way=way):
                for c in halo(field, r, way):
                    c.wait_send()

    loads[0].wait()
    send_halos(now, 0)

    loads[1].wait()
    eye = iota((length, length), 0) == iota((length, length), 1)
    cols = []
    for t in range(steps):
        col = jnp.sum(jnp.where(eye, weights[t : t + 1, :], 0.0), axis=1, keepdims=True)
        cols.append([jnp.where(home[0] == slab * slots + s, col, 0.0) for s in range(slots)])

    def offered(face, t):
        at = pl.ds(pl.multiple_of(face * pts, 128), pts)
        total = cols[t][0] * slabs[pl.ds(0, length), at]
        for s in range(1, slots):
            total = total + cols[t][s] * slabs[pl.ds(s * length, length), at]
        return jnp.sum(total, axis=0, keepdims=True)

    face_x = jnp.where(box == 0, 0, 1)
    face_z = jnp.where(slab == 0, 2, 3)
    common = [offered(f, t) for f in (face_x, 4, 5) for t in range(steps)]
    for kind in range(2):
        vsend[kind] = jnp.concatenate(common + [offered(2 + kind, t) for t in range(steps)], axis=0)

    def give(d):
        peer = lax.rem(slab + d, n_slab)
        return pltpu.make_async_remote_copy(
            vsend.at[jnp.where(peer == 0, 0, 1)], vrecv.at[d - 1], vs_sem.at[d - 1], vr_sem.at[d - 1],
            device_id={"slab": peer}, device_id_type=MESH)

    for d in range(1, n_slab):
        give(d).start()

    loads[3].wait()
    bank, total_z = prof.shape
    here = iota((wz, total_z), 1) == slab * wz + iota((wz, total_z), 0)
    for m in reversed(range(members)):
        mine = jnp.sum(jnp.where(iota((bank, total_z), 0) == ids[m], prof[...], 0.0), axis=0, keepdims=True)
        gain = 1.0 + jnp.sum(jnp.where(here, mine, 0.0), axis=1, keepdims=True)
        for x in range(wx):
            coef[pl.ds((m * wx + x) * wz, wz), :] = coef[pl.ds(x * wz, wz), :] * gain

    z_at, y_at = iota((wz, ny), 0), iota((wz, ny), 1)

    def advance(field, before, out):
        def member(m, carry):
            base = m * block
            for x in range(wx):
                rows = pl.ds(pl.multiple_of(base + x * wz, 8), wz)
                c = field[rows, :]
                lap = -6.0 * c
                if x > 0:
                    lap = lap + field[pl.ds(pl.multiple_of(base + (x - 1) * wz, 8), wz), :]
                if x < wx - 1:
                    lap = lap + field[pl.ds(pl.multiple_of(base + (x + 1) * wz, 8), wz), :]
                lap = lap + jnp.where(z_at == 0, 0.0, pltpu.roll(c, 1, 0))
                lap = lap + jnp.where(z_at == wz - 1, 0.0, pltpu.roll(c, wz - 1, 0))
                lap = lap + jnp.where(y_at == 0, 0.0, pltpu.roll(c, 1, 1))
                lap = lap + jnp.where(y_at == ny - 1, 0.0, pltpu.roll(c, ny - 1, 1))
                out[rows, :] = (2.0 * c - before[rows, :]) + coef[rows, :] * lap
            return carry

        lax.fori_loop(0, members, member, 0)

    loads[2].wait()
    advance(now, prev, one)

    def where_is(face):
        cell = cells[pl.ds(face, 1), :]
        cx = quotient(cell, total_z * ny)
        rest = cell - cx * (total_z * ny)
        cz = quotient(rest, ny)
        return cx - box * wx, cz - slab * wz, rest - cz * ny

    for d in range(1, n_slab):
        give(d).wait_recv()
    values = vsend[jnp.where(slab == 0, 0, 1)]
    for d in range(1, n_slab):
        values = values + vrecv[d - 1]

    def rows_of(k):
        return [values[2 * k + t : 2 * k + t + 1] for t in range(steps)]

    ax, az, ay = where_is(face_x)
    on_x = place(wz, az, (ax >= 0) & (ax < wx), rows_of(0), ny, ay)
    ax, az, ay = where_is(face_z)
    on_z = place(wx, ax, (az >= 0) & (az < wz), rows_of(3), ny, ay)
    wide = 128
    sides = []
    for k, face in ((1, 4), (2, 5)):
        ax, az, ay = where_is(face)
        sides.append(place(wz, az, (ax >= 0) & (ax < wx), rows_of(k), wide, ax))
    plane_x = jnp.where(box == 0, 0, wx - 1)
    row_z = jnp.where(slab == 0, 0, wz - 1)

    def add_source(t, out):
        lane = iota((wz, 128), 1)
        for x in range(wx):
            low = jnp.where(lane == 0, sides[0][t][:, x : x + 1], 0.0)
            high = jnp.where(lane == 127, sides[1][t][:, x : x + 1], 0.0)
            depth = jnp.where(z_at == row_z, on_z[t][x : x + 1, :], 0.0)
            for m in range(members):
                rows = pl.ds((m * wx + x) * wz, wz)
                out[rows, :] += depth
                out[rows, pl.ds(0, 128)] += low
                out[rows, pl.ds(ny - 128, 128)] += high
        for m in range(members):
            rows = pl.ds(pl.multiple_of((m * wx + plane_x) * wz, 8), wz)
            out[rows, :] += on_x[t]

    add_source(0, one)
    add_halos(now, 0, one)

    send_halos(one, 1)
    advance(one, now, two)
    add_source(1, two)
    add_halos(one, 1, two)
    end_sends(now, 0)
    end_sends(one, 1)
    for d in range(1, n_slab):
        give(d).wait_send()


def on_device(pressure_now, pressure_prev, courant_sq, member_profiles, member_ids, stored_slabs,
              slab_home, interp_weights, surface_cells):
    members, wx, wz, ny = pressure_now.shape
    slots, length, points = stored_slabs.shape
    pts = surface_cells.shape[1]
    n_box, n_slab = lax.axis_size("box"), lax.axis_size("slab")
    dims = (members, wx, wz, ny, slots, length, pts, n_box, n_slab)
    rows = members * wx * wz
    vmem = pl.BlockSpec(memory_space=pltpu.VMEM)
    smem = pl.BlockSpec(memory_space=pltpu.SMEM)
    hbm = pl.BlockSpec(memory_space=pltpu.HBM)
    field = jax.ShapeDtypeStruct((rows, ny), F32)
    dma = pltpu.SemaphoreType.DMA
    new, last = pl.pallas_call(
        functools.partial(kernel, dims),
        out_shape=(field, field),
        in_specs=[smem, smem, vmem, vmem, vmem, hbm, hbm, hbm, hbm],
        out_specs=(vmem, vmem),
        scratch_shapes=[pltpu.VMEM((rows, ny), F32)] * 3
        + [
            pltpu.VMEM((slots * length, points), F32),
            pltpu.VMEM((2, 2, members, wx, ny), F32),
            pltpu.VMEM((2, 2, members, wz, ny), F32),
            pltpu.VMEM((2, 2, members, wx, ny), F32),
            pltpu.VMEM((2, 8, pts), F32),
            pltpu.VMEM((n_slab - 1, 8, pts), F32),
            dma((4,)), dma((2, 4, members)), dma((2, 4, members)),
            dma((n_slab - 1,)), dma((n_slab - 1,)),
        ],
        compiler_params=pltpu.CompilerParams(collective_id=0, has_side_effects=True,
                                             vmem_limit_bytes=32 * 1024 * 1024),
    )(
        member_ids, slab_home, member_profiles, interp_weights, surface_cells,
        pressure_now.reshape(rows, ny), pressure_prev.reshape(rows, ny),
        courant_sq.reshape(wx * wz, ny), stored_slabs.reshape(slots * length, points),
    )
    return new.reshape(pressure_now.shape), last.reshape(pressure_now.shape)


def solution(mesh):
    in_specs = (
        P("ens", "box", "slab", None), P("ens", "box", "slab", None), P("box", "slab", None), P(),
        P("ens"), P("slab", None, None), P("ens"), P(), P(),
    )
    out_specs = (P("ens", "box", "slab", None), P("ens", "box", "slab", None))
    return jax.shard_map(on_device, mesh=mesh, in_specs=in_specs, out_specs=out_specs, check_vma=False)
```

time: 110 us -> 21.2 us (0.19)
  other arithmetic: 68.5 us -> 0 us
  starting transfers between devices: 21.8 us -> 0 us
  Pallas kernels: 0 us -> 12.3 us
  blocking collectives: 11.1 us -> 0 us
  local copies, waits for them, and re-layouts: 3.01 us -> 7.18 us
  waiting for transfers between devices: 1.59 us -> 0 us
  matrix products: 1.2 us -> 0 us
    scatter-add x2 -> x0, other arithmetic: 65.4 us -> none  [inject(): jnp.zeros((volume,), jnp.float32).at[target].add(point_values, mode='drop')]
    ppermute x8 -> x0, starting transfers between devices: 21.8 us -> none  [the longest x4 16.5 us: extended(): before = lax.ppermute(last, axis, up)]
    pallas_call x0 -> x1, Pallas kernels: none -> 12.3 us  [on_device(): pl.pallas_call(functools.partial(kernel, dims), out_shape=(field, field),...]
    psum x1 -> x0, blocking collectives: 11.1 us -> none  [on_device(): values = lax.psum(offered, 'slab')]
    unnamed x23 -> x18, local copies, waits for them, and re-layouts: 1.26 us -> 7.18 us
    add x3 -> x0, other arithmetic: 2.57 us -> none  [the longest x2 2.5 us: inject(): return field + source.reshape(extent_x, extent_z, depth_y)[None]]
    ppermute x8 -> x0, waiting for transfers between devices: 1.59 us -> none  [the longest x4 1.31 us: extended(): before = lax.ppermute(last, axis, up)]
    slice x4 -> x0, local copies, waits for them, and re-layouts: 1.59 us -> none  [the longest x2 0.94 us: extended(): leading = lax.slice_in_dim(array, 0, width, axis=dim)]
  transfers between devices with their start and end apart: 8 -> 0, of which waited for: 2 -> 0; matrix products, arithmetic and copies ran while one was open for 62% -> 0% of each run, Pallas kernels for 0% -> 0%
where the time goes in v1:
time: 21.2 us; the launch traced here: 20.8 us
  Pallas kernels  12.3 us (58%)
  local copies, waits for them, and re-layouts  7.18 us (34%)
  between operations  1.32 us (6%)
    pallas_call x1, Pallas kernels, on_device(): pl.pallas_call(functools.partial(kernel, dims), out_shape=(field, field),...  12.3 us
    unnamed x18, local copies, waits for them, and re-layouts  7.18 us

profile of v1, /device:TPU:0, one launch (start us, length us, event | category | flops | bytes accessed | tf_op | source)
XLA Modules:
  0.0 20.8 jit_solution(8979903018290695970)
XLA Ops:
  1.3 0.0 copy-start.5
  1.3 0.0 copy-start.6
  1.3 0.0 copy-start.7
  1.3 0.7 %copy-done.5 = f32[8,64]{1,0:T(8,128)S(1)} copy-done((f32[8,64]{1,0:T(8,128)S(1)}, f32[8,64]{1,0:T(8,128)}, u32[]{:S(2)}) %copy-start.5) | copy-done | bytes 2072
  2.0 0.0 copy-done.6
  2.0 0.0 copy-done.7
  2.0 0.0 copy-start
  2.0 1.1 %copy-done = f32[2,16,6144]{2,1,0:T(8,128)S(1)} copy-done((f32[2,16,6144]{2,1,0:T(8,128)S(1)}, f32[2,16,6144]{2,1,0:T(8,128)}, u32[]{:S(2)}) %copy-start) | copy-done | bytes 786456
  3.1 0.0 copy-start.1
  3.1 1.0 %copy-done.1 = f32[2,16,16,256]{3,2,1,0:T(8,128)S(1)} copy-done((f32[2,16,16,256]{3,2,1,0:T(8,128)S(1)}, f32[2,16,16,256]{3,2,1,0:T(8,128)}, u32[]{:S(2)}) %copy-start.1) | copy-done | bytes 524312
  4.2 0.0 copy-start.2
  4.2 1.0 %copy-done.2 = f32[2,16,16,256]{3,2,1,0:T(8,128)S(1)} copy-done((f32[2,16,16,256]{3,2,1,0:T(8,128)S(1)}, f32[2,16,16,256]{3,2,1,0:T(8,128)}, u32[]{:S(2)}) %copy-start.2) | copy-done | bytes 524312
  5.2 0.0 copy-start.3
  5.2 0.9 %copy-done.3 = f32[16,16,256]{2,1,0:T(8,128)S(1)} copy-done((f32[16,16,256]{2,1,0:T(8,128)S(1)}, f32[16,16,256]{2,1,0:T(8,128)}, u32[]{:S(2)}) %copy-start.3) | copy-done | bytes 262168
  6.1 0.0 copy-start.4
  6.1 0.8 %copy-done.4 = s32[6,1024]{1,0:T(8,128)S(1)} copy-done((s32[6,1024]{1,0:T(8,128)S(1)}, s32[6,1024]{1,0:T(8,128)}, u32[]{:S(2)}) %copy-start.4) | copy-done | bytes 24600
  6.9 12.3 %shard_map.104 = (f32[512,256]{1,0:T(8,128)S(1)}, f32[512,256]{1,0:T(8,128)S(1)}) custom-call(s32[2]{0:T(128)S(1)} %copy-done.7, s32[1]{0:T(128)S(6)} %copy.13.home, f32[8,64]{1,0:T(8,128)S(1)} %copy-done.5, f32[2,16]{1,0:T(2,128)S(1)} %copy-done.6, s32[6,1024]{1,0:T(8,128)S(1)} %copy-done.4, f32[512,256]{1,0:T(8,128)S(1)} %bitcast.7, ...), custom_call_target="tpu_custom_call" | custom-call | tf_op jit(solution)/shard_map/pallas_call | solution.py:283
  19.2 0.8 %copy.14 = f32[2,16,16,256]{3,2,1,0:T(8,128)} copy(f32[2,16,16,256]{3,2,1,0:T(8,128)S(1)} %bitcast.10) | data formatting | bytes 1048576
  20.0 0.8 %copy.15 = f32[2,16,16,256]{3,2,1,0:T(8,128)} copy(f32[2,16,16,256]{3,2,1,0:T(8,128)S(1)} %bitcast.9) | data formatting | bytes 1048576
Async XLA Ops:
  1.3 0.7 %copy-start.5 = (f32[8,64]{1,0:T(8,128)S(1)}, f32[8,64]{1,0:T(8,128)}, u32[]{:S(2)}) copy-start(f32[8,64]{1,0:T(8,128)} %prof.1) | copy-start | bytes 6148
  1.3 0.7 %copy-start.6 = (f32[2,16]{1,0:T(2,128)S(1)}, f32[2,16]{1,0:T(2,128)}, u32[]{:S(2)}) copy-start(f32[2,16]{1,0:T(2,128)} %weights.1) | copy-start | bytes 388
  1.3 0.7 %copy-start.7 = (s32[2]{0:T(128)S(1)}, s32[2]{0:T(128)}, u32[]{:S(2)}) copy-start(s32[2]{0:T(128)} %ids.1) | copy-start | bytes 28
  2.0 1.1 %copy-start = (f32[2,16,6144]{2,1,0:T(8,128)S(1)}, f32[2,16,6144]{2,1,0:T(8,128)}, u32[]{:S(2)}) copy-start(f32[2,16,6144]{2,1,0:T(8,128)} %param.14) | copy-start | bytes 2359300
  3.1 1.0 %copy-start.1 = (f32[2,16,16,256]{3,2,1,0:T(8,128)S(1)}, f32[2,16,16,256]{3,2,1,0:T(8,128)}, u32[]{:S(2)}) copy-start(f32[2,16,16,256]{3,2,1,0:T(8,128)} %param.9) | copy-start | bytes 1572868
  4.2 1.0 %copy-start.2 = (f32[2,16,16,256]{3,2,1,0:T(8,128)S(1)}, f32[2,16,16,256]{3,2,1,0:T(8,128)}, u32[]{:S(2)}) copy-start(f32[2,16,16,256]{3,2,1,0:T(8,128)} %param.10) | copy-start | bytes 1572868
  5.2 0.9 %copy-start.3 = (f32[16,16,256]{2,1,0:T(8,128)S(1)}, f32[16,16,256]{2,1,0:T(8,128)}, u32[]{:S(2)}) copy-start(f32[16,16,256]{2,1,0:T(8,128)} %param.11) | copy-start | bytes 786436
  6.1 0.8 %copy-start.4 = (s32[6,1024]{1,0:T(8,128)S(1)}, s32[6,1024]{1,0:T(8,128)}, u32[]{:S(2)}) copy-start(s32[6,1024]{1,0:T(8,128)} %cells.1) | copy-start | bytes 73732

commit v2 on v1

--- a/solution.py
+++ b/solution.py
@@ -28,14 +28,13 @@
     return high, mid, rest - mid
 
 
-def place(rows, row_of, valid, per_step, cols, col_of):
+def place(rows, row_of, valid, per_step, right):
     hit = (iota((rows, row_of.shape[1]), 0) == row_of) & valid
     parts = []
     for v in per_step:
         for term in split3(v):
             parts.append(jnp.where(hit, term, 0.0).astype(BF16))
     left = jnp.concatenate(parts, axis=0)
-    right = jnp.where(iota((cols, col_of.shape[1]), 0) == col_of, 1.0, 0.0).astype(BF16)
     sums = lax.dot_general(left, right, (((1,), (1,)), ((), ())), preferred_element_type=F32)
     out = []
     for t in range(len(per_step)):
@@ -46,20 +45,13 @@
     return out
 
 
-def kernel(dims, ids, home, prof, weights, cells, now_h, prev_h, cour_h, slabs_h, two, one,
-           now, prev, coef, slabs, zsend, xghost, zghost, vsend, vrecv,
-           load_sem, hs_sem, hr_sem, vs_sem, vr_sem):
+def kernel(dims, home, ids_h, prof_h, weights_h, cells_h, now_h, prev_h, cour_h, slabs_h, two, one,
+           ids, prof, weights, cells, now, prev, coef, slabs, xsend, zsend, xghost, zghost, xextra, zextra,
+           hot_x, hot_z, hot_low, hot_high, vsend, vrecv, load_sem, hs_sem, hr_sem, vs_sem, vr_sem):
     members, wx, wz, ny, slots, length, pts, n_box, n_slab = dims
     steps = 2
     block = wx * wz
     box, slab = lax.axis_index("box"), lax.axis_index("slab")
-    loads = [
-        pltpu.make_async_copy(src, dst, load_sem.at[i])
-        for i, (src, dst) in enumerate(((now_h, now), (slabs_h, slabs), (prev_h, prev), (cour_h, coef.at[pl.ds(0, block)])))
-    ]
-    for c in loads:
-        c.start()
-
     barrier = pltpu.get_barrier_semaphore()
 
     def greet(target):
@@ -75,16 +67,23 @@
 
     for d in range(1, n_slab):
         greet({"slab": lax.rem(slab + d, n_slab)})
-    box_peers = jnp.where(box > 0, 1, 0) + jnp.where(box < n_box - 1, 1, 0)
-    pl.semaphore_wait(barrier, n_slab - 1 + box_peers)
-
-    def halo(field, r, way):
+    pairs = ((now_h, now), (slabs_h, slabs), (weights_h, weights), (cour_h, coef.at[pl.ds(0, block)]),
+             (prof_h, prof), (ids_h, ids), (prev_h, prev), (cells_h, cells))
+    loads = [pltpu.make_async_copy(src, dst, load_sem.at[i]) for i, (src, dst) in enumerate(pairs)]
+    for c in loads:
+        c.start()
+
+    def source(r, way, m):
+        if r > 0:
+            return xsend.at[way, m]
+        return now.at[pl.ds((m * wx + (wx - 1 if way == 0 else 0)) * wz, wz)]
+
+    def halo(r, way):
         if way < 2:
-            plane = wx - 1 if way == 0 else 0
             peer = {"box": box + 1 if way == 0 else box - 1}
             return [
                 pltpu.make_async_remote_copy(
-                    field.at[pl.ds((m * wx + plane) * wz, wz)], xghost.at[r, way, m],
+                    source(r, way, m), xghost.at[r, way, m],
                     hs_sem.at[r, way, m], hr_sem.at[r, way, m], device_id=peer, device_id_type=MESH)
                 for m in range(members)
             ]
@@ -98,57 +97,68 @@
     sends_to = (box < n_box - 1, box > 0, slab < n_slab - 1, slab > 0)
     hears_from = (box > 0, box < n_box - 1, slab > 0, slab < n_slab - 1)
 
-    def send_halos(field, r):
-        for way in (0, 1):
+    def pack(field, r):
+        for m in range(members):
+            if r > 0:
+                for way in (0, 1):
+                    plane = wx - 1 if way == 0 else 0
+                    xsend[way, m] = field[pl.ds((m * wx + plane) * wz, wz), :]
+            for way in (2, 3):
+                row = wz - 1 if way == 2 else 0
+                for x in range(wx):
+                    zsend[r, way - 2, m, x : x + 1, :] = field[pl.ds((m * wx + x) * wz + row, 1), :]
+
+    def send_halos(r):
+        for way in range(4):
             @pl.when(sends_to[way])
             def _(way=way):
-                for c in halo(field, r, way):
+                for c in halo(r, way):
                     c.start()
-        for way in (2, 3):
-            row = wz - 1 if way == 2 else 0
-            for m in range(members):
-                for x in range(wx):
-                    zsend[r, way - 2, m, x : x + 1, :] = field[pl.ds((m * wx + x) * wz + row, 1), :]
-
-            @pl.when(sends_to[way])
-            def _(way=way):
-                for c in halo(field, r, way):
-                    c.start()
-
-    def add_halos(field, r, out):
+
+    def add_halos(r, out):
         for way in (0, 1):
             plane = 0 if way == 0 else wx - 1
 
             @pl.when(hears_from[way])
             def _(way=way, plane=plane):
-                for m, c in enumerate(halo(field, r, way)):
+                for m, c in enumerate(halo(r, way)):
                     c.wait_recv()
                 for m in range(members):
                     rows = pl.ds((m * wx + plane) * wz, wz)
-                    out[rows, :] += coef[rows, :] * xghost[r, way, m]
+                    ghost = xghost[r, way, m]
+                    if r > 0:
+                        ghost = ghost + xextra[way]
+                    out[rows, :] += coef[rows, :] * ghost
         for way in (2, 3):
             row = 0 if way == 2 else wz - 1
 
             @pl.when(hears_from[way])
             def _(way=way, row=row):
-                for c in halo(field, r, way):
+                for c in halo(r, way):
                     c.wait_recv()
                 for m in range(members):
                     for x in range(wx):
                         at = pl.ds((m * wx + x) * wz + row, 1)
-                        out[at, :] += coef[at, :] * zghost[r, way - 2, m, x : x + 1, :]
-
-    def end_sends(field, r):
+                        ghost = zghost[r, way - 2, m, x : x + 1, :]
+                        if r > 0:
+                            ghost = ghost + zextra[way - 2, x : x + 1, :]
+                        out[at, :] += coef[at, :] * ghost
+
+    def end_sends(r):
         for way in range(4):
             @pl.when(sends_to[way])
             def _(way=way):
-                for c in halo(field, r, way):
+                for c in halo(r, way):
                     c.wait_send()
 
     loads[0].wait()
-    send_halos(now, 0)
-
-    loads[1].wait()
+    pack(now, 0)
+    box_peers = jnp.where(box > 0, 1, 0) + jnp.where(box < n_box - 1, 1, 0)
+    pl.semaphore_wait(barrier, n_slab - 1 + box_peers)
+    send_halos(0)
+
+    for i in (1, 2):
+        loads[i].wait()
     eye = iota((length, length), 0) == iota((length, length), 1)
     cols = []
     for t in range(steps):
@@ -177,7 +187,8 @@
     for d in range(1, n_slab):
         give(d).start()
 
-    loads[3].wait()
+    for i in (3, 4, 5):
+        loads[i].wait()
     bank, total_z = prof.shape
     here = iota((wz, total_z), 1) == slab * wz + iota((wz, total_z), 0)
     for m in reversed(range(members)):
@@ -208,8 +219,11 @@
 
         lax.fori_loop(0, members, member, 0)
 
-    loads[2].wait()
+    loads[6].wait()
     advance(now, prev, one)
+
+    loads[7].wait()
+    margin, wide = 8, 128
 
     def where_is(face):
         cell = cells[pl.ds(face, 1), :]
@@ -218,6 +232,28 @@
         cz = quotient(rest, ny)
         return cx - box * wx, cz - slab * wz, rest - cz * ny
 
+    def hot(cols, col_of):
+        return jnp.where(iota((cols, pts), 0) == col_of, 1.0, 0.0).astype(BF16)
+
+    px, pz, py = where_is(face_x)
+    px_valid = (px >= 0) & (px < wx)
+    px_row = pz + margin
+    hot_x[...] = hot(ny, py)
+    px, pz, py = where_is(face_z)
+    pz_valid = (pz >= 0) & (pz < wz)
+    pz_row = px + margin
+    hot_z[...] = hot(ny, py)
+    px, pz, py = where_is(4)
+    low_row = pz + margin
+    hot_low[...] = hot(wide, px + margin)
+    px, pz, py = where_is(5)
+    high_row = pz + margin
+    hot_high[...] = hot(wide, px + margin)
+
+    add_halos(0, one)
+    pack(one, 1)
+    send_halos(1)
+
     for d in range(1, n_slab):
         give(d).wait_recv()
     values = vsend[jnp.where(slab == 0, 0, 1)]
@@ -227,42 +263,43 @@
     def rows_of(k):
         return [values[2 * k + t : 2 * k + t + 1] for t in range(steps)]
 
-    ax, az, ay = where_is(face_x)
-    on_x = place(wz, az, (ax >= 0) & (ax < wx), rows_of(0), ny, ay)
-    ax, az, ay = where_is(face_z)
-    on_z = place(wx, ax, (az >= 0) & (az < wz), rows_of(3), ny, ay)
-    wide = 128
-    sides = []
-    for k, face in ((1, 4), (2, 5)):
-        ax, az, ay = where_is(face)
-        sides.append(place(wz, az, (ax >= 0) & (ax < wx), rows_of(k), wide, ax))
+    tall_x, tall_z = wx + 2 * margin, wz + 2 * margin
+    always = low_row >= -tall_z * n_slab * pts
+    on_x = place(tall_z, px_row, px_valid, rows_of(0), hot_x[...])
+    on_z = place(tall_x, pz_row, pz_valid, rows_of(3), hot_z[...])
+    low_y = place(tall_z, low_row, always, rows_of(1), hot_low[...])
+    high_y = place(tall_z, high_row, always, rows_of(2), hot_high[...])
     plane_x = jnp.where(box == 0, 0, wx - 1)
-    row_z = jnp.where(slab == 0, 0, wz - 1)
+    row_z = jnp.where(slab == 0, 0, wz - 1) + margin
+    tall_row, tall_lane = iota((tall_z, ny), 0), iota((tall_z, ny), 1)
+
+    def source_plane(t, x):
+        at = x + margin
+        out = jnp.where(tall_row == row_z, on_z[t][at : at + 1, :], 0.0)
+        out = out + jnp.where(tall_lane == 0, low_y[t][:, at : at + 1], 0.0)
+        out = out + jnp.where(tall_lane == ny - 1, high_y[t][:, at : at + 1], 0.0)
+        if x in (0, wx - 1):
+            out = out + jnp.where(plane_x == x, on_x[t], 0.0)
+        return out
 
     def add_source(t, out):
-        lane = iota((wz, 128), 1)
         for x in range(wx):
-            low = jnp.where(lane == 0, sides[0][t][:, x : x + 1], 0.0)
-            high = jnp.where(lane == 127, sides[1][t][:, x : x + 1], 0.0)
-            depth = jnp.where(z_at == row_z, on_z[t][x : x + 1, :], 0.0)
+            plane = source_plane(t, x)
+            if t == 0:
+                zextra[0, x : x + 1, :] = plane[margin - 1 : margin]
+                zextra[1, x : x + 1, :] = plane[margin + wz : margin + wz + 1]
             for m in range(members):
-                rows = pl.ds((m * wx + x) * wz, wz)
-                out[rows, :] += depth
-                out[rows, pl.ds(0, 128)] += low
-                out[rows, pl.ds(ny - 128, 128)] += high
-        for m in range(members):
-            rows = pl.ds(pl.multiple_of((m * wx + plane_x) * wz, 8), wz)
-            out[rows, :] += on_x[t]
+                out[pl.ds((m * wx + x) * wz, wz), :] += plane[margin : margin + wz]
+        if t == 0:
+            xextra[0] = source_plane(t, -1)[margin : margin + wz]
+            xextra[1] = source_plane(t, wx)[margin : margin + wz]
 
     add_source(0, one)
-    add_halos(now, 0, one)
-
-    send_halos(one, 1)
     advance(one, now, two)
     add_source(1, two)
-    add_halos(one, 1, two)
-    end_sends(now, 0)
-    end_sends(one, 1)
+    add_halos(1, two)
+    end_sends(0)
+    end_sends(1)
     for d in range(1, n_slab):
         give(d).wait_send()
 
@@ -276,33 +313,40 @@
     dims = (members, wx, wz, ny, slots, length, pts, n_box, n_slab)
     rows = members * wx * wz
     vmem = pl.BlockSpec(memory_space=pltpu.VMEM)
-    smem = pl.BlockSpec(memory_space=pltpu.SMEM)
+    in_hbm = lambda a: pltpu.with_memory_space_constraint(a, pltpu.HBM)
     hbm = pl.BlockSpec(memory_space=pltpu.HBM)
     field = jax.ShapeDtypeStruct((rows, ny), F32)
     dma = pltpu.SemaphoreType.DMA
     new, last = pl.pallas_call(
         functools.partial(kernel, dims),
         out_shape=(field, field),
-        in_specs=[smem, smem, vmem, vmem, vmem, hbm, hbm, hbm, hbm],
+        in_specs=[pl.BlockSpec(memory_space=pltpu.SMEM)] + [hbm] * 8,
         out_specs=(vmem, vmem),
-        scratch_shapes=[pltpu.VMEM((rows, ny), F32)] * 3
-        + [
+        scratch_shapes=[
+            pltpu.SMEM(member_ids.shape, I32),
+            pltpu.VMEM(member_profiles.shape, F32), pltpu.VMEM(interp_weights.shape, F32),
+            pltpu.VMEM(surface_cells.shape, I32),
+            pltpu.VMEM((rows, ny), F32), pltpu.VMEM((rows, ny), F32), pltpu.VMEM((rows, ny), F32),
             pltpu.VMEM((slots * length, points), F32),
+            pltpu.VMEM((2, members, wz, ny), F32),
             pltpu.VMEM((2, 2, members, wx, ny), F32),
             pltpu.VMEM((2, 2, members, wz, ny), F32),
             pltpu.VMEM((2, 2, members, wx, ny), F32),
+            pltpu.VMEM((2, wz, ny), F32), pltpu.VMEM((2, wx, ny), F32),
+            pltpu.VMEM((ny, pts), BF16), pltpu.VMEM((ny, pts), BF16),
+            pltpu.VMEM((128, pts), BF16), pltpu.VMEM((128, pts), BF16),
             pltpu.VMEM((2, 8, pts), F32),
             pltpu.VMEM((n_slab - 1, 8, pts), F32),
-            dma((4,)), dma((2, 4, members)), dma((2, 4, members)),
+            dma((8,)), dma((2, 4, members)), dma((2, 4, members)),
             dma((n_slab - 1,)), dma((n_slab - 1,)),
         ],
         compiler_params=pltpu.CompilerParams(collective_id=0, has_side_effects=True,
                                              vmem_limit_bytes=32 * 1024 * 1024),
-    )(
-        member_ids, slab_home, member_profiles, interp_weights, surface_cells,
+    )(slab_home, *(in_hbm(a) for a in (
+        member_ids, member_profiles, interp_weights, surface_cells,
         pressure_now.reshape(rows, ny), pressure_prev.reshape(rows, ny),
         courant_sq.reshape(wx * wz, ny), stored_slabs.reshape(slots * length, points),
-    )
+    )))
     return new.reshape(pressure_now.shape), last.reshape(pressure_now.shape)
 
 

time: 21.2 us -> 13.6 us (0.64); the launches traced: 20.8 us -> 13.5 us
  local copies, waits for them, and re-layouts: 7.18 us -> 1.59 us
  Pallas kernels: 12.3 us -> 10.6 us
    unnamed x18 -> x2, local copies, waits for them, and re-layouts: 7.18 us -> 1.59 us
    pallas_call x1, Pallas kernels: 12.3 us -> 10.6 us  [on_device(): pl.pallas_call(functools.partial(kernel, dims), out_shape=(field, field),...]
where the time goes in v2:
time: 13.6 us; the launch traced here: 13.5 us
  Pallas kernels  10.6 us (78%)
  local copies, waits for them, and re-layouts  1.59 us (12%)
  between operations  1.29 us (9%)
    pallas_call x1, Pallas kernels, on_device(): pl.pallas_call(functools.partial(kernel, dims), out_shape=(field, field),...  10.6 us
    unnamed x2, local copies, waits for them, and re-layouts  1.59 us

profile of v2, /device:TPU:0, one launch (start us, length us, event | category | flops | bytes accessed | tf_op | source)
XLA Modules:
  0.0 13.5 jit_solution(7869873343468162915)
XLA Ops:
  1.3 10.6 %shard_map.104 = (f32[512,256]{1,0:T(8,128)S(1)}, f32[512,256]{1,0:T(8,128)S(1)}) custom-call(s32[1]{0:T(128)S(6)} %copy.13.home, s32[2]{0:T(128)} %ids_h.1, f32[8,64]{1,0:T(8,128)} %prof_h.1, f32[2,16]{1,0:T(2,128)} %weights_h.1, s32[6,1024]{1,0:T(8,128)} %cells_h.1, f32[512,256]{1,0:T(8,128)} %bitcast.9, f32[512,256]{1,0:T(8,128)} %bitcast.10, ...), custom_call_target="tpu_custom_call" | custom-call | tf_op jit(solution)/shard_map/pallas_call | solution.py:320
  11.9 0.8 %copy.14 = f32[2,16,16,256]{3,2,1,0:T(8,128)} copy(f32[2,16,16,256]{3,2,1,0:T(8,128)S(1)} %bitcast.7) | data formatting | bytes 1048576
  12.7 0.8 %copy.15 = f32[2,16,16,256]{3,2,1,0:T(8,128)} copy(f32[2,16,16,256]{3,2,1,0:T(8,128)S(1)} %bitcast.6) | data formatting | bytes 1048576

commit v3 on v2

--- a/solution.py
+++ b/solution.py
@@ -52,6 +52,11 @@
     steps = 2
     block = wx * wz
     box, slab = lax.axis_index("box"), lax.axis_index("slab")
+    pairs = ((now_h, now), (slabs_h, slabs), (weights_h, weights), (cour_h, coef.at[pl.ds(0, block)]),
+             (prof_h, prof), (ids_h, ids), (prev_h, prev), (cells_h, cells))
+    loads = [pltpu.make_async_copy(src, dst, load_sem.at[i]) for i, (src, dst) in enumerate(pairs)]
+    loads[0].start()
+
     barrier = pltpu.get_barrier_semaphore()
 
     def greet(target):
@@ -67,10 +72,7 @@
 
     for d in range(1, n_slab):
         greet({"slab": lax.rem(slab + d, n_slab)})
-    pairs = ((now_h, now), (slabs_h, slabs), (weights_h, weights), (cour_h, coef.at[pl.ds(0, block)]),
-             (prof_h, prof), (ids_h, ids), (prev_h, prev), (cells_h, cells))
-    loads = [pltpu.make_async_copy(src, dst, load_sem.at[i]) for i, (src, dst) in enumerate(pairs)]
-    for c in loads:
+    for c in loads[1:]:
         c.start()
 
     def source(r, way, m):
@@ -302,6 +304,14 @@
     end_sends(1)
     for d in range(1, n_slab):
         give(d).wait_send()
+
+
+def store_kernel(two, one, next_h, last_h, sem):
+    copies = [pltpu.make_async_copy(src, dst, sem.at[i]) for i, (src, dst) in enumerate(((two, next_h), (one, last_h)))]
+    for c in copies:
+        c.start()
+    for c in copies:
+        c.wait()
 
 
 def on_device(pressure_now, pressure_prev, courant_sq, member_profiles, member_ids, stored_slabs,
@@ -347,6 +357,15 @@
         pressure_now.reshape(rows, ny), pressure_prev.reshape(rows, ny),
         courant_sq.reshape(wx * wz, ny), stored_slabs.reshape(slots * length, points),
     )))
+    placed = pltpu.HBM((rows, ny), F32)
+    new, last = pl.pallas_call(
+        store_kernel,
+        out_shape=(placed, placed),
+        in_specs=[vmem, vmem],
+        out_specs=(hbm, hbm),
+        scratch_shapes=[dma((2,))],
+        compiler_params=pltpu.CompilerParams(vmem_limit_bytes=4 * 1024 * 1024),
+    )(new, last)
     return new.reshape(pressure_now.shape), last.reshape(pressure_now.shape)
 
 

time: 13.6 us -> 13 us (0.956)
  local copies, waits for them, and re-layouts: 1.59 us -> 0 us
  Pallas kernels: 10.6 us -> 11.6 us
    unnamed x2 -> x0, local copies, waits for them, and re-layouts: 1.59 us -> none
    pallas_call x0 -> x1, Pallas kernels: none -> 0.99 us  [on_device(): pl.pallas_call(store_kernel, out_shape=(placed, placed), in_specs=[vmem,...]
where the time goes in v3:
time: 13 us; the launch traced here: 12.9 us
  Pallas kernels  11.6 us (89%)
  between operations  1.29 us (10%)
    pallas_call x1, Pallas kernels, on_device(): pl.pallas_call(functools.partial(kernel, dims), out_shape=(field, field),...  10.6 us
    pallas_call x1, Pallas kernels, on_device(): pl.pallas_call(store_kernel, out_shape=(placed, placed), in_specs=[vmem,...  0.99 us

profile of v3, /device:TPU:0, one launch (start us, length us, event | category | flops | bytes accessed | tf_op | source)
XLA Modules:
  0.0 12.9 jit_solution(13516608304437720889)
XLA Ops:
  1.3 10.6 %shard_map.104 = (f32[512,256]{1,0:T(8,128)S(1)}, f32[512,256]{1,0:T(8,128)S(1)}) custom-call(s32[1]{0:T(128)S(6)} %copy.11.home, s32[2]{0:T(128)} %ids_h.1, f32[8,64]{1,0:T(8,128)} %prof_h.1, f32[2,16]{1,0:T(2,128)} %weights_h.1, s32[6,1024]{1,0:T(8,128)} %cells_h.1, f32[512,256]{1,0:T(8,128)} %bitcast.7, f32[512,256]{1,0:T(8,128)} %bitcast.8, ...), custom_call_target="tpu_custom_call" | custom-call | tf_op jit(solution)/shard_map/pallas_call | solution.py:330
  11.9 1.0 %shard_map.105 = (f32[512,256]{1,0:T(8,128)}, f32[512,256]{1,0:T(8,128)}) custom-call(f32[512,256]{1,0:T(8,128)S(1)} %get-tuple-element.6.two, f32[512,256]{1,0:T(8,128)S(1)} %get-tuple-element.7.one), custom_call_target="tpu_custom_call" | custom-call | tf_op jit(solution)/shard_map/pallas_call | solution.py:361

commit v4 on v3

--- a/solution.py
+++ b/solution.py
@@ -72,8 +72,8 @@
 
     for d in range(1, n_slab):
         greet({"slab": lax.rem(slab + d, n_slab)})
-    for c in loads[1:]:
-        c.start()
+    for i in (1, 2):
+        loads[i].start()
 
     def source(r, way, m):
         if r > 0:
@@ -158,6 +158,8 @@
     box_peers = jnp.where(box > 0, 1, 0) + jnp.where(box < n_box - 1, 1, 0)
     pl.semaphore_wait(barrier, n_slab - 1 + box_peers)
     send_halos(0)
+    for i in (3, 4, 5, 6, 7):
+        loads[i].start()
 
     for i in (1, 2):
         loads[i].wait()

time: 13 us -> 13 us (level)
  no operation moved by 1% of the time
where the time goes in v4:
time: 13 us; the launch traced here: 12.9 us
  Pallas kernels  11.6 us (89%)
  between operations  1.29 us (10%)
    pallas_call x1, Pallas kernels, on_device(): pl.pallas_call(functools.partial(kernel, dims), out_shape=(field, field),...  10.6 us
    pallas_call x1, Pallas kernels, on_device(): pl.pallas_call(store_kernel, out_shape=(placed, placed), in_specs=[vmem,...  0.99 us

profile of v4, /device:TPU:0, one launch (start us, length us, event | category | flops | bytes accessed | tf_op | source)
XLA Modules:
  0.0 12.9 jit_solution(11828542031367342075)
XLA Ops:
  1.3 10.6 %shard_map.104 = (f32[512,256]{1,0:T(8,128)S(1)}, f32[512,256]{1,0:T(8,128)S(1)}) custom-call(s32[1]{0:T(128)S(6)} %copy.11.home, s32[2]{0:T(128)} %ids_h.1, f32[8,64]{1,0:T(8,128)} %prof_h.1, f32[2,16]{1,0:T(2,128)} %weights_h.1, s32[6,1024]{1,0:T(8,128)} %cells_h.1, f32[512,256]{1,0:T(8,128)} %bitcast.7, f32[512,256]{1,0:T(8,128)} %bitcast.8, ...), custom_call_target="tpu_custom_call" | custom-call | tf_op jit(solution)/shard_map/pallas_call | solution.py:332
  11.9 1.0 %shard_map.105 = (f32[512,256]{1,0:T(8,128)}, f32[512,256]{1,0:T(8,128)}) custom-call(f32[512,256]{1,0:T(8,128)S(1)} %get-tuple-element.6.two, f32[512,256]{1,0:T(8,128)S(1)} %get-tuple-element.7.one), custom_call_target="tpu_custom_call" | custom-call | tf_op jit(solution)/shard_map/pallas_call | solution.py:363
